TPU v7x, 256 devices: a whole 4x4x8 slice. The times are simulated.
256 devices in a mesh: outer: 16 (over z_lo, x), inner: 16 (over y, z_hi, core).
Axes of the slice: x: 4, y: 4, z: 8 (z_hi: 2, z_lo: 4; z = z_hi * 4 + z_lo), core: 2. Of those that a mesh axis runs over, the one named last changes fastest.
Arguments:
- queries: bfloat16 [8192, 2, 4096], P('outer', None, 'inner'), may hold values from -52 to 52
- keys: bfloat16 [8192, 2, 4096], P('outer', None, 'inner'), may hold values from -6 to 6
- values: bfloat16 [8192, 2, 4096], P('outer', None, 'inner'), may hold values from -6 to 6
Outputs:
- attended: bfloat16 [8192, 2, 4096], P(('outer', 'inner'))
All inputs are finite; a program needn't handle non-finite values.
Results may differ from a plain program's by a relative error of at most 0.004.
Values may be sent and summed in bfloat16 or wider, within the bound.
No kernel may reach another device: no remote copies, remote signals or barrier semaphores. Data moves between devices by JAX's collectives and lax.ppermute only.
A program may use at most 128 MiB of HBM per device.

v0:
```python
from functools import partial
import math

import jax
import jax.numpy as jnp
from jax import lax
from jax.sharding import PartitionSpec as P

HEAD_DIM = 128


def attend_keys(running, key_block, value_block, query_heads, head_count):
    peak_rows, totals, numerator = running
    key_count = key_block.shape[0]
    key_heads = key_block.reshape(key_count, head_count, HEAD_DIM)
    value_heads = value_block.reshape(key_count, head_count, HEAD_DIM)
    scores = jnp.einsum(
        "qhd,khd->qhk", query_heads, key_heads, preferred_element_type=jnp.float32
    ) * (1.0 / math.sqrt(HEAD_DIM))
    new_peaks = jnp.maximum(peak_rows, jnp.max(scores, axis=2))
    shrink = jnp.exp(peak_rows - new_peaks)
    weights = jnp.exp(scores - new_peaks[..., None])
    totals = totals * shrink + jnp.sum(weights, axis=2)
    numerator = numerator * shrink[..., None] + jnp.einsum(
        "qhk,khd->qhd",
        weights.astype(jnp.bfloat16),
        value_heads,
        preferred_element_type=jnp.float32,
    )
    return (new_peaks, totals, numerator)


def attend_piece(running, pieces, start_row, query_part, head_count):
    key_rows, value_rows = pieces
    row_count = query_part.shape[0]
    query_heads = query_part.reshape(row_count, head_count, HEAD_DIM)
    block_count = key_rows.shape[0] // row_count
    key_blocks = key_rows.reshape(block_count, row_count, key_rows.shape[1])
    value_blocks = value_rows.reshape(block_count, row_count, value_rows.shape[1])

    def one_block(state, blocks):
        return (attend_keys(state, blocks[0], blocks[1], query_heads, head_count), None)

    running, unused = lax.scan(one_block, running, (key_blocks, value_blocks))
    return running


def start_state(row_count, head_count):
    peak_rows = jnp.full((row_count, head_count), -1e30, jnp.float32)
    totals = jnp.zeros((row_count, head_count), jnp.float32)
    numerator = jnp.zeros((row_count, head_count, HEAD_DIM), jnp.float32)
    return (peak_rows, totals, numerator)


def finish_state(running):
    peak_rows, totals, numerator = running
    averaged = numerator / totals[..., None]
    return averaged.reshape(numerator.shape[0], -1).astype(jnp.bfloat16)


def flatten(array):
    return array.reshape(array.shape[0], array.shape[1] * array.shape[2])


def per_device(queries, keys, values):
    tok_rows, networks, local_cols = queries.shape
    flat_queries, flat_keys, flat_values = (flatten(queries), flatten(keys), flatten(values))
    head_count = networks * local_cols // HEAD_DIM
    folder = partial(attend_piece, query_part=flat_queries, head_count=head_count)
    running = folder(
        start_state(tok_rows, head_count),
        (
            lax.all_gather(flat_keys, "outer", axis=0, tiled=True),
            lax.all_gather(flat_values, "outer", axis=0, tiled=True),
        ),
        jnp.int32(0),
    )
    local_out = finish_state(running).reshape(tok_rows, networks, local_cols)
    attended = lax.all_to_all(local_out, "inner", split_axis=0, concat_axis=2, tiled=True)
    return attended


def solution(mesh):
    return jax.shard_map(
        per_device,
        mesh=mesh,
        in_specs=(P("outer", None, "inner"), P("outer", None, "inner"), P("outer", None, "inner")),
        out_specs=P(("outer", "inner"), None, None),
        check_vma=False,
    )
```

profile of v0, /device:TPU:32, one launch (start us, length us, event | category | flops | bytes accessed | tf_op | source)
XLA Modules:
  0.0 320.9 jit_solution(2837683536750189921)
XLA Ops:
  6.5 1.9 copy.35
  8.5 1.9 copy.36
  10.5 1.3 copy.21
  12.1 99.0 %all-gather.3.cloned.1.call-done = bf16[8192,512]{1,0:T(8,128)(2,1)} async-done(((bf16[512,512]{1,0:T(8,128)(2,1)}), bf16[8192,512]{1,0:T(8,128)(2,1)}) %all-gather.3.cloned.1.call-update) | async-done | bytes 8388624 | tf_op jit(solution)/shard_map/all_gather | solution.py:73
  111.1 101.0 %all-gather.5.cloned.1.call-done = bf16[8192,512]{1,0:T(8,128)(2,1)} async-done(((bf16[512,512]{1,0:T(8,128)(2,1)}), bf16[8192,512]{1,0:T(8,128)(2,1)}) %all-gather.5.cloned.1.call-update) | async-done | bytes 8388624 | tf_op jit(solution)/shard_map/all_gather | solution.py:74
  212.0 70.4 %while.15 = (s32[]{:T(128)}, f32[512,4]{0,1:T(4,128)S(1)}, f32[512,4]{0,1:T(4,128)S(1)}, f32[512,4,128]{0,2,1:T(8,128)S(1)}, bf16[16,512,512]{2,1,0:T(8,128)(2,1...) while((s32[]{:T(128)}, f32[512,4]{0,1:T(4,128)S(1)}, ...), condition=%wide.region_3.4_spmd.clone, body=%wide.region_0.3_spmd.clone.sunk | while | flops 546056192 | bytes 20578420 | solution.py:44
  212.0 1.3 constant_dynamic-slice_fusion.3
  215.2 1.1 fusion.31
  216.4 1.3 constant_dynamic-slice_fusion.3
  219.6 1.1 fusion.31
  220.8 1.3 constant_dynamic-slice_fusion.3
  224.1 1.1 fusion.31
  225.2 1.3 constant_dynamic-slice_fusion.3
  229.6 1.3 constant_dynamic-slice_fusion.3
  232.9 1.1 fusion.31
  234.0 1.3 constant_dynamic-slice_fusion.3
  237.3 1.1 fusion.31
  238.4 1.3 constant_dynamic-slice_fusion.3
  241.7 1.1 fusion.31
  242.8 1.3 constant_dynamic-slice_fusion.3
  246.1 1.1 fusion.31
  247.3 1.3 constant_dynamic-slice_fusion.3
  250.5 1.1 fusion.31
  251.7 1.3 constant_dynamic-slice_fusion.3
  254.9 1.1 fusion.31
  256.1 1.3 constant_dynamic-slice_fusion.3
  260.5 1.3 constant_dynamic-slice_fusion.3
  264.9 1.3 constant_dynamic-slice_fusion.3
  269.3 1.3 constant_dynamic-slice_fusion.3
  273.7 1.3 constant_dynamic-slice_fusion.3
  278.1 1.3 constant_dynamic-slice_fusion.3
  283.1 29.7 %all_to_all.18 = bf16[512,2,256]{2,1,0:T(2,128)(2,1)S(1)} all-to-all(bf16[512,2,256]{2,1,0:T(2,128)(2,1)S(1)} %copy.25), channel_id=1, replica_groups=mesh['outer'=16,'inner'=16] {'inner'}, dimensions={0} | all-to-all | bytes 1048576 | tf_op jit(solution)/shard_map/all_to_all | solution.py:79
  (132 shorter events, 41.2 us)
Async XLA Ops:
  6.5 104.5 %all-gather.3.cloned.1.call-start = ((), (), s32[]{:S(2)}) async-start(), calls=%async_computation.1 | async-start | bytes 8912896 | tf_op jit(solution)/shard_map/all_gather | solution.py:73
  8.5 203.5 %all-gather.5.cloned.1.call-start = ((), (), s32[]{:S(2)}) async-start(), calls=%async_computation.2 | async-start | bytes 8912896 | tf_op jit(solution)/shard_map/all_gather | solution.py:74
Sparse Core Ops, SparseCore 0:
  9.1 101.9 all-gather.2
  112.9 99.1 all-gather.4
where the time goes:
time: 322 us; the launch traced here: 321 us
  waiting for transfers between devices  200 us (62%)
  local copies, waits for them, and re-layouts  34.4 us (11%)
  matrix products  30.6 us (10%)
  blocking collectives  29.7 us (9%)
  between operations  13.5 us (4%)
  other arithmetic  11.9 us (4%)
    all_gather x1, waiting for transfers between devices, per_device(): lax.all_gather(flat_values, 'outer', axis=0, tiled=True)  101 us
    all_gather x1, waiting for transfers between devices, per_device(): lax.all_gather(flat_keys, 'outer', axis=0, tiled=True)  99 us
    all_to_all x1, blocking collectives, per_device(): lax.all_to_all(local_out, 'inner', split_axis=0, concat_axis=2, tiled=True)  29.7 us
    dynamic_slice x48, local copies, waits for them, and re-layouts, attend_piece(): running, unused = lax.scan(one_block, running, (key_blocks, value_blocks))  27.2 us
    dot_general x16, matrix products, attend_keys(): jnp.einsum('qhk,khd->qhd', weights.astype(jnp.bfloat16), value_heads, pre...  18.3 us
    dot_general x16, matrix products, attend_keys(): jnp.einsum('qhd,khd->qhk', query_heads, key_heads, preferred_element_type...  12.4 us
    reduce_sum x16, other arithmetic, attend_keys(): totals = totals * shrink + jnp.sum(weights, axis=2)  11.3 us
  transfers between devices with their start and end apart: 2, of which 2 were waited for; matrix products, arithmetic and copies ran while one was open for 1% of the time, Pallas kernels for 0%

commit v1 on v0

v1 whole, which is shorter than its diff:
```python
from functools import partial
import math

import jax
import jax.numpy as jnp
from jax import lax
from jax.experimental import pallas as pl
from jax.experimental.pallas import tpu as pltpu
from jax.sharding import Mesh, PartitionSpec as P


HEAD_DIM = 128
LOG2_SCALE = math.log2(math.e) / math.sqrt(HEAD_DIM)
SUM_ROWS = 16
PIECE = 256
Q_TILE = 512
VMEM_BYTES = 24 * 1024 * 1024


def pack_kernel(zl_ref, q_ref, k_ref, v_ref, *out_refs):
    for s in range(4):
        q_out, c0_out, c1_out = out_refs[3 * s:3 * s + 3]
        at = pl.multiple_of(lax.rem(zl_ref[0] + s, 4) * HEAD_DIM, HEAD_DIM)
        head = pl.ds(at, HEAD_DIM)
        q_out[...] = q_ref[:, head]
        c0_out[0] = k_ref[0:PIECE, head]
        c0_out[1] = v_ref[0:PIECE, head]
        c1_out[0] = k_ref[PIECE:, head]
        c1_out[1] = v_ref[PIECE:, head]


def pack_heads(zl, queries, keys, values):
    rows = queries.shape[0]
    flat = [a.reshape(rows, 4 * HEAD_DIM) for a in (queries, keys, values)]
    vmem = pl.BlockSpec(memory_space=pltpu.VMEM)
    kv_shape = jax.ShapeDtypeStruct((2, PIECE, HEAD_DIM), jnp.bfloat16)
    q_shape = jax.ShapeDtypeStruct((rows, HEAD_DIM), jnp.bfloat16)
    outs = pl.pallas_call(
        pack_kernel,
        in_specs=[pl.BlockSpec(memory_space=pltpu.SMEM), vmem, vmem, vmem],
        out_specs=[vmem] * 12,
        out_shape=[q_shape, kv_shape, kv_shape] * 4,
        compiler_params=pltpu.CompilerParams(vmem_limit_bytes=VMEM_BYTES),
        name="pack",
    )(zl, *flat)
    return outs[0::3], outs[1::3], outs[2::3]


def flash_kernel(first, last, counts, zl_ref, q_ref, *refs):
    kv_refs, refs = refs[: len(counts)], refs[len(counts):]
    if not first:
        peak_in, acc_in, *refs = refs
    if last:
        out_ref, vt_ref = refs
    else:
        peak_out, acc_out, vt_ref = refs
    pieces = [(ref, p) for ref, count in zip(kv_refs, counts) for p in range(count)]

    @pl.when(pl.program_id(0) == 0)
    def _():
        for at, (ref, p) in enumerate(pieces):
            vt_ref[0:HEAD_DIM, at * PIECE:(at + 1) * PIECE] = ref[p, 1].T
        vt_ref[HEAD_DIM:, :] = jnp.ones((SUM_ROWS, vt_ref.shape[1]), jnp.bfloat16)

    queries = q_ref[0]
    tile = queries.shape[0]
    if first:
        peak = jnp.full((1, tile), -1e30, jnp.float32)
        acc = jnp.zeros((HEAD_DIM + SUM_ROWS, tile), jnp.float32)
    else:
        peak = peak_in[0:1, :]
        acc = acc_in[...]

    def score(at):
        keys = jnp.concatenate([ref[p, 0] for ref, p in pieces[at:at + 2]], axis=0)
        return lax.dot_general(
            keys, queries, (((1,), (1,)), ((), ())), preferred_element_type=jnp.float32
        )

    scores = score(0)
    for at in range(0, len(pieces), 2):
        following = score(at + 2) if at + 2 < len(pieces) else None
        new_peak = jnp.maximum(peak, jnp.max(scores, axis=0, keepdims=True))
        shift = new_peak * LOG2_SCALE
        weights = jnp.exp2(scores * LOG2_SCALE - shift).astype(jnp.bfloat16)
        shrink = jnp.exp2(peak * LOG2_SCALE - shift)
        acc = acc * shrink + jnp.dot(
            vt_ref[:, at * PIECE:(at + 2) * PIECE], weights, preferred_element_type=jnp.float32
        )
        peak, scores = new_peak, following
    if last:
        attended = acc[0:HEAD_DIM, :] / acc[HEAD_DIM:HEAD_DIM + 1, :]
        out_ref[0] = attended.T.astype(jnp.bfloat16)
    else:
        peak_out[...] = jnp.broadcast_to(peak, peak_out.shape)
        acc_out[...] = acc


def flash(zl, queries, blocks, state, last):
    sources, rows, _ = queries.shape
    per_source = rows // Q_TILE
    total = sources * rows
    counts = tuple(b.shape[0] for b in blocks)
    first = state is None
    q_spec = pl.BlockSpec((1, Q_TILE, HEAD_DIM), lambda i, z: (i // per_source, i % per_source, 0))
    in_specs = [q_spec] + [
        pl.BlockSpec((c, 2, PIECE, HEAD_DIM), lambda i, z: (0, 0, 0, 0)) for c in counts
    ]
    peak_spec = pl.BlockSpec((8, Q_TILE), lambda i, z: (0, i))
    acc_spec = pl.BlockSpec((HEAD_DIM + SUM_ROWS, Q_TILE), lambda i, z: (0, i))
    args = [queries, *blocks]
    if not first:
        in_specs += [peak_spec, acc_spec]
        args += list(state)
    if last:
        out_specs = pl.BlockSpec(
            (1, Q_TILE, HEAD_DIM),
            lambda i, z: (lax.rem(z[0] + 4 - i // per_source, 4), i % per_source, 0),
        )
        out_shape = jax.ShapeDtypeStruct(queries.shape, jnp.bfloat16)
    else:
        out_specs = [peak_spec, acc_spec]
        out_shape = [
            jax.ShapeDtypeStruct((8, total), jnp.float32),
            jax.ShapeDtypeStruct((HEAD_DIM + SUM_ROWS, total), jnp.float32),
        ]
    key_count = sum(counts) * PIECE
    return pl.pallas_call(
        partial(flash_kernel, first, last, counts),
        grid_spec=pltpu.PrefetchScalarGridSpec(
            num_scalar_prefetch=1,
            grid=(total // Q_TILE,),
            in_specs=in_specs,
            out_specs=out_specs,
            scratch_shapes=[pltpu.VMEM((HEAD_DIM + SUM_ROWS, key_count), jnp.bfloat16)],
        ),
        out_shape=out_shape,
        compiler_params=pltpu.CompilerParams(
            dimension_semantics=("arbitrary",), vmem_limit_bytes=VMEM_BYTES
        ),
        cost_estimate=pl.CostEstimate(
            flops=16 * total * key_count * HEAD_DIM,
            bytes_accessed=2 * (total + 2 * key_count) * HEAD_DIM,
            transcendentals=total * key_count,
        ),
        name="flash",
    )(zl, *args)


def shift(array, axis, by):
    return lax.ppermute(array, axis, [(i, (i + by) % 4) for i in range(4)])


def to_heads(packed):
    parts = [packed[0]]
    for s in (1, 2, 3):
        parts.append(shift(packed[s], "zl", s))
    return jnp.stack(parts)


def around_ring(block):
    left = shift(block, "x", 1)
    right = shift(block, "x", -1)
    half = block.shape[0] // 2
    far_a = shift(left[:half], "x", 1)
    far_b = shift(right[half:], "x", -1)
    return left, right, [far_a, far_b]


def attention(queries, keys, values):
    rows = queries.shape[0]
    zl = lax.axis_index("zl").astype(jnp.int32).reshape(1)
    q_packed, c0, c1 = pack_heads(zl, queries, keys, values)
    own0 = to_heads(c0)
    q_all = to_heads(q_packed)
    own1 = to_heads(c1)
    left0, right0, far0 = around_ring(own0)
    left1, right1, far1 = around_ring(own1)
    steps = [
        ("own0", [own0]), ("left0", [left0]), ("right0", [right0]), ("far0", far0),
        ("own1", [own1]), ("near1", [left1, right1]), ("far1", far1),
    ]
    state = None
    for name, blocks in steps:
        state = flash(zl, q_all, blocks, state, name == "far1")
    blocks = state.reshape(64, rows // 16, HEAD_DIM)
    blocks = lax.all_to_all(blocks, ("zl", "y", "zh", "c"), 0, 0, tiled=True)
    out = blocks.reshape(2, 2, 16, rows // 16, HEAD_DIM).transpose(3, 0, 2, 1, 4)
    return out.reshape(rows // 16, 2, 32 * HEAD_DIM)


def solution(mesh):
    grid = Mesh(mesh.devices.reshape(4, 4, 4, 2, 2), ("zl", "x", "y", "zh", "c"))
    spec = P(("zl", "x"), None, ("y", "zh", "c"))
    return jax.shard_map(
        attention,
        mesh=grid,
        in_specs=(spec, spec, spec),
        out_specs=P(("zl", "x", "y", "zh", "c"), None, None),
        check_vma=False,
    )
```

time: 322 us -> 126 us (0.39)
  waiting for transfers between devices: 200 us -> 28.6 us
  Pallas kernels: 0 us -> 33.5 us
  local copies, waits for them, and re-layouts: 34.4 us -> 2.95 us
  matrix products: 30.6 us -> 0 us
  starting transfers between devices: 0.04 us -> 29.5 us
  between operations: 13.5 us -> 0.18 us
  other arithmetic: 11.9 us -> 0.2 us
    all_gather x2 -> x0, waiting for transfers between devices: 200 us -> none  [the longest x1 101 us: per_device(): lax.all_gather(flat_values, 'outer', axis=0, tiled=True)]
    pallas_call x0 -> x8, Pallas kernels: none -> 33.5 us  [the longest x7 33.2 us: flash(): pl.pallas_call(partial(flash_kernel, first, last, counts), grid_spec=pltp...]
    dot_general x32 -> x0, matrix products: 30.6 us -> none  [the longest x16 18.3 us: attend_keys(): jnp.einsum('qhk,khd->qhd', weights.astype(jnp.bfloat16), value_heads, pre...]
    ppermute x0 -> x17, starting transfers between devices: none -> 29.5 us  [shift(): return lax.ppermute(array, axis, [(i, (i + by) % 4) for i in range(4)])]
    ppermute x0 -> x17, waiting for transfers between devices: none -> 28.6 us  [shift(): return lax.ppermute(array, axis, [(i, (i + by) % 4) for i in range(4)])]
    dynamic_slice x48 -> x0, local copies, waits for them, and re-layouts: 27.2 us -> none  [attend_piece(): running, unused = lax.scan(one_block, running, (key_blocks, value_blocks))]
    reduce_sum x16 -> x0, other arithmetic: 11.3 us -> none  [attend_keys(): totals = totals * shrink + jnp.sum(weights, axis=2)]
    unnamed x4 -> x7, local copies, waits for them, and re-layouts: 5.43 us -> 1.42 us
  transfers between devices with their start and end apart: 2 -> 17, of which waited for: 2 -> 9; matrix products, arithmetic and copies ran while one was open for 1% -> 0% of each run, Pallas kernels for 0% -> 23%
where the time goes in v1:
time: 126 us; the launch traced here: 124 us
  Pallas kernels  33.5 us (27%)
  blocking collectives  29.6 us (23%)
  starting transfers between devices  29.5 us (23%)
  waiting for transfers between devices  28.6 us (23%)
  local copies, waits for them, and re-layouts  2.95 us (2%)
    pallas_call x7, Pallas kernels, flash(): pl.pallas_call(partial(flash_kernel, first, last, counts), grid_spec=pltp...  33.2 us
    all_to_all x1, blocking collectives, attention(): blocks = lax.all_to_all(blocks, ('zl', 'y', 'zh', 'c'), 0, 0, tiled=True)  29.6 us
    ppermute x17, starting transfers between devices, shift(): return lax.ppermute(array, axis, [(i, (i + by) % 4) for i in range(4)])  29.5 us
    ppermute x17, waiting for transfers between devices, shift(): return lax.ppermute(array, axis, [(i, (i + by) % 4) for i in range(4)])  28.6 us
  transfers between devices with their start and end apart: 17, of which 9 were waited for; matrix products, arithmetic and copies ran while one was open for 0% of the time, Pallas kernels for 23%

profile of v1, /device:TPU:32, one launch (start us, length us, event | category | flops | bytes accessed | tf_op | source)
XLA Modules:
  0.0 124.4 jit_solution(445392843793206469)
XLA Ops:
  0.0 1.2 copy.5
  1.7 2.0 %collective-permute-start.10 = (bf16[2,256,128]{2,1,0:T(8,128)(2,1)S(1)}, bf16[2,256,128]{2,1,0:T(8,128)(2,1)S(1)}, u32[]{:S(2)}, u32[]{:S(2)}) collective-permute-start(bf16[2,256,128]{2,1,0:T(8,128)(2,1)S(1)} %get-tuple-element.38), channel_id=1, source_target_pairs={{0,64},{64,128},{128,192},{192,0},{1,65},{65,129},{129,193},{193,1... | collective-permute-start | bytes 393224 | tf_op jit(solution)/shard_map/ppermute | solution.py:151
  3.7 2.3 %collective-permute-start.11 = (bf16[2,256,128]{2,1,0:T(8,128)(2,1)S(1)}, bf16[2,256,128]{2,1,0:T(8,128)(2,1)S(1)}, u32[]{:S(2)}, u32[]{:S(2)}) collective-permute-start(bf16[2,256,128]{2,1,0:T(8,128)(2,1)S(1)} %get-tuple-element.39), channel_id=1, source_target_pairs={{0,128},{64,192},{128,0},{192,64},{1,129},{65,193},{129,1},{193,65... | collective-permute-start | bytes 393224 | tf_op jit(solution)/shard_map/ppermute | solution.py:151
  6.0 1.1 collective-permute-start.12
  7.1 0.9 collective-permute-start.3
  8.0 2.5 %collective-permute-start.4 = (bf16[2,256,128]{2,1,0:T(8,128)(2,1)S(1)}, bf16[2,256,128]{2,1,0:T(8,128)(2,1)S(1)}, u32[]{:S(2)}, u32[]{:S(2)}) collective-permute-start(bf16[2,256,128]{2,1,0:T(8,128)(2,1)S(1)} %get-tuple-element.35), channel_id=1, source_target_pairs={{0,128},{64,192},{128,0},{192,64},{1,129},{65,193},{129,1},{193,65... | collective-permute-start | bytes 393224 | tf_op jit(solution)/shard_map/ppermute | solution.py:151
  10.5 2.2 %collective-permute-done.10 = bf16[2,256,128]{2,1,0:T(8,128)(2,1)S(1)} collective-permute-done((bf16[2,256,128]{2,1,0:T(8,128)(2,1)S(1)}, bf16[2,256,128]{2,1,0:T(8,128)(2,1)S(1)}, u32[]{:S(2)}, u32[]{:S(2)}) %collective-permute-start.10) | collective-permute-done | bytes 131104 | tf_op jit(solution)/shard_map/ppermute | solution.py:151
  12.7 8.4 %collective-permute-done.11 = bf16[2,256,128]{2,1,0:T(8,128)(2,1)S(1)} collective-permute-done((bf16[2,256,128]{2,1,0:T(8,128)(2,1)S(1)}, bf16[2,256,128]{2,1,0:T(8,128)(2,1)S(1)}, u32[]{:S(2)}, u32[]{:S(2)}) %collective-permute-start.11) | collective-permute-done | bytes 131104 | tf_op jit(solution)/shard_map/ppermute | solution.py:151
  21.2 3.0 %collective-permute-done.12 = bf16[2,256,128]{2,1,0:T(8,128)(2,1)S(1)} collective-permute-done((bf16[2,256,128]{2,1,0:T(8,128)(2,1)S(1)}, bf16[2,256,128]{2,1,0:T(8,128)(2,1)S(1)}, u32[]{:S(2)}, u32[]{:S(2)}) %collective-permute-start.12) | collective-permute-done | bytes 131104 | tf_op jit(solution)/shard_map/ppermute | solution.py:151
  24.1 0.9 collective-permute-start.1
  25.0 2.0 %collective-permute-start.2 = (bf16[512,128]{1,0:T(8,128)(2,1)S(1)}, bf16[512,128]{1,0:T(8,128)(2,1)S(1)}, u32[]{:S(2)}, u32[]{:S(2)}) collective-permute-start(bf16[512,128]{1,0:T(8,128)(2,1)S(1)} %get-tuple-element.32), channel_id=1, source_target_pairs={{0,192},{64,0},{128,64},{192,128},{1,193},{65,1},{129,65},{193,129... | collective-permute-start | bytes 393224 | tf_op jit(solution)/shard_map/ppermute | solution.py:151
  27.1 5.8 %collective-permute-done.4 = bf16[2,256,128]{2,1,0:T(8,128)(2,1)S(1)} collective-permute-done((bf16[2,256,128]{2,1,0:T(8,128)(2,1)S(1)}, bf16[2,256,128]{2,1,0:T(8,128)(2,1)S(1)}, u32[]{:S(2)}, u32[]{:S(2)}) %collective-permute-start.4) | collective-permute-done | bytes 131104 | tf_op jit(solution)/shard_map/ppermute | solution.py:151
  32.9 1.5 %collective-permute-start.13 = (bf16[4,2,256,128]{3,2,1,0:T(8,128)(2,1)S(1)}, bf16[4,2,256,128]{3,2,1,0:T(8,128)(2,1)S(1)}, u32[]{:S(2)}, u32[]{:S(2)}) collective-permute-start(bf16[4,2,256,128]{3,2,1,0:T(8,128)(2,1)S(1)} %pad_maximum_fusion.2.refs_0_), channel_id=1, source_target_pairs={{0,16},{16,32},{32,48},{48,0},{1,17},{17,33},{33,49},{49,1},{2,18}... | collective-permute-start | bytes 1572872 | tf_op jit(solution)/shard_map/ppermute | solution.py:151
  34.4 2.4 %collective-permute-start.15 = (bf16[4,2,256,128]{3,2,1,0:T(8,128)(2,1)S(1)}, bf16[4,2,256,128]{3,2,1,0:T(8,128)(2,1)S(1)}, u32[]{:S(2)}, u32[]{:S(2)}) collective-permute-start(bf16[4,2,256,128]{3,2,1,0:T(8,128)(2,1)S(1)} %pad_maximum_fusion.2.refs_0_), channel_id=1, source_target_pairs={{0,48},{16,0},{32,16},{48,32},{1,49},{17,1},{33,17},{49,33},{2,50}... | collective-permute-start | bytes 1572872 | tf_op jit(solution)/shard_map/ppermute | solution.py:151
  37.4 2.8 %collective-permute-start.8 = (bf16[4,2,256,128]{3,2,1,0:T(8,128)(2,1)S(1)}, bf16[4,2,256,128]{3,2,1,0:T(8,128)(2,1)S(1)}, u32[]{:S(2)}, u32[]{:S(2)}) collective-permute-start(bf16[4,2,256,128]{3,2,1,0:T(8,128)(2,1)S(1)} %pad_maximum_fusion.1.refs_0_), channel_id=1, source_target_pairs={{0,48},{16,0},{32,16},{48,32},{1,49},{17,1},{33,17},{49,33},{2,50}... | collective-permute-start | bytes 1572872 | tf_op jit(solution)/shard_map/ppermute | solution.py:151
  40.3 4.1 %flash.7 = (f32[8,2048]{1,0:T(8,128)S(1)}, f32[144,2048]{1,0:T(8,128)S(1)}) custom-call(s32[1]{0:T(128)} %bitcast.zl_ref, bf16[4,512,128]{2,1,0:T(8,128)(2,1)S(1)} %pad_maximum_fusion.q_ref, bf16[4,2,256,128]{3,2,1,0:T(8,128)(2,1)S(1)} %pad_maximum_fusion.2.refs_0_), custom_call_target="tpu_custom_call" | custom-call | flops 4294967296 | bytes 1048576 | tf_op jit(solution)/shard_map/flash/pallas_call | solution.py:128
  44.3 1.8 %collective-permute-done.13.refs_0_ = bf16[4,2,256,128]{3,2,1,0:T(8,128)(2,1)S(1)} collective-permute-done((bf16[4,2,256,128]{3,2,1,0:T(8,128)(2,1)S(1)}, bf16[4,2,256,128]{3,2,1,0:T(8,128)(2,1)S(1)}, u32[]{:S(2)}, u32[]{:S(2)}) %collective-permute-start.13) | collective-permute-done | bytes 524320 | tf_op jit(solution)/shard_map/ppermute | solution.py:151
  46.2 1.6 %collective-permute-start.14 = (bf16[2,2,256,128]{3,2,1,0:T(8,128)(2,1)S(1)}, bf16[2,2,256,128]{3,2,1,0:T(8,128)(2,1)S(1)}, u32[]{:S(2)}, u32[]{:S(2)}) collective-permute-start(bf16[2,2,256,128]{3,2,1,0:T(8,128)(2,1)S(1)} %slice.18), channel_id=1, source_target_pairs={{0,16},{16,32},{32,48},{48,0},{1,17},{17,33},{33,49},{49,1},{2,18}... | collective-permute-start | bytes 786440 | tf_op jit(solution)/shard_map/ppermute | solution.py:151
  47.8 1.4 %collective-permute-done.15.refs_0_ = bf16[4,2,256,128]{3,2,1,0:T(8,128)(2,1)S(1)} collective-permute-done((bf16[4,2,256,128]{3,2,1,0:T(8,128)(2,1)S(1)}, bf16[4,2,256,128]{3,2,1,0:T(8,128)(2,1)S(1)}, u32[]{:S(2)}, u32[]{:S(2)}) %collective-permute-start.15) | collective-permute-done | bytes 524320 | tf_op jit(solution)/shard_map/ppermute | solution.py:151
  49.2 3.9 %collective-permute-start.16 = (bf16[2,2,256,128]{3,2,1,0:T(8,128)(2,1)S(1)}, bf16[2,2,256,128]{3,2,1,0:T(8,128)(2,1)S(1)}, u32[]{:S(2)}, u32[]{:S(2)}) collective-permute-start(bf16[2,2,256,128]{3,2,1,0:T(8,128)(2,1)S(1)} %slice.19), channel_id=1, source_target_pairs={{0,48},{16,0},{32,16},{48,32},{1,49},{17,1},{33,17},{49,33},{2,50}... | collective-permute-start | bytes 786440 | tf_op jit(solution)/shard_map/ppermute | solution.py:151
  53.1 4.3 %collective-permute-done.6.refs_0_ = bf16[4,2,256,128]{3,2,1,0:T(8,128)(2,1)S(1)} collective-permute-done((bf16[4,2,256,128]{3,2,1,0:T(8,128)(2,1)S(1)}, bf16[4,2,256,128]{3,2,1,0:T(8,128)(2,1)S(1)}, u32[]{:S(2)}, u32[]{:S(2)}) %collective-permute-start.6) | collective-permute-done | bytes 524320 | tf_op jit(solution)/shard_map/ppermute | solution.py:151
  57.4 1.6 %collective-permute-start.7 = (bf16[2,2,256,128]{3,2,1,0:T(8,128)(2,1)S(1)}, bf16[2,2,256,128]{3,2,1,0:T(8,128)(2,1)S(1)}, u32[]{:S(2)}, u32[]{:S(2)}) collective-permute-start(bf16[2,2,256,128]{3,2,1,0:T(8,128)(2,1)S(1)} %slice.16), channel_id=1, source_target_pairs={{0,16},{16,32},{32,48},{48,0},{1,17},{17,33},{33,49},{49,1},{2,18}... | collective-permute-start | bytes 786440 | tf_op jit(solution)/shard_map/ppermute | solution.py:151
  59.0 1.4 %collective-permute-done.8.refs_1_ = bf16[4,2,256,128]{3,2,1,0:T(8,128)(2,1)S(1)} collective-permute-done((bf16[4,2,256,128]{3,2,1,0:T(8,128)(2,1)S(1)}, bf16[4,2,256,128]{3,2,1,0:T(8,128)(2,1)S(1)}, u32[]{:S(2)}, u32[]{:S(2)}) %collective-permute-start.8) | collective-permute-done | bytes 524320 | tf_op jit(solution)/shard_map/ppermute | solution.py:151
  60.5 3.7 %collective-permute-start.9 = (bf16[2,2,256,128]{3,2,1,0:T(8,128)(2,1)S(1)}, bf16[2,2,256,128]{3,2,1,0:T(8,128)(2,1)S(1)}, u32[]{:S(2)}, u32[]{:S(2)}) collective-permute-start(bf16[2,2,256,128]{3,2,1,0:T(8,128)(2,1)S(1)} %slice.17), channel_id=1, source_target_pairs={{0,48},{16,0},{32,16},{48,32},{1,49},{17,1},{33,17},{49,33},{2,50}... | collective-permute-start | bytes 786440 | tf_op jit(solution)/shard_map/ppermute | solution.py:151
  64.1 4.3 %flash.8 = (f32[8,2048]{1,0:T(8,128)S(1)}, f32[144,2048]{1,0:T(8,128)S(1)}) custom-call(s32[1]{0:T(128)} %bitcast.zl_ref, bf16[4,512,128]{2,1,0:T(8,128)(2,1)S(1)} %pad_maximum_fusion.q_ref, bf16[4,2,256,128]{3,2,1,0:T(8,128)(2,1)S(1)} %collective-permute-done.13.refs_0_, f32[8,2048]{1,0:T(8,128)S(1)} %get-tuple-element.41.refs_1_, ...), custom_call_target="tpu_custom_call" | custom-call | flops 4294967296 | bytes 1048576 | tf_op jit(solution)/shard_map/flash/pallas_call | solution.py:128
  68.4 4.3 %flash.9 = (f32[8,2048]{1,0:T(8,128)S(1)}, f32[144,2048]{1,0:T(8,128)S(1)}) custom-call(s32[1]{0:T(128)} %bitcast.zl_ref, bf16[4,512,128]{2,1,0:T(8,128)(2,1)S(1)} %pad_maximum_fusion.q_ref, bf16[4,2,256,128]{3,2,1,0:T(8,128)(2,1)S(1)} %collective-permute-done.15.refs_0_, f32[8,2048]{1,0:T(8,128)S(1)} %get-tuple-element.43.refs_1_, ...), custom_call_target="tpu_custom_call" | custom-call | flops 4294967296 | bytes 1048576 | tf_op jit(solution)/shard_map/flash/pallas_call | solution.py:128
  72.7 4.3 %flash.10 = (f32[8,2048]{1,0:T(8,128)S(1)}, f32[144,2048]{1,0:T(8,128)S(1)}) custom-call(s32[1]{0:T(128)} %bitcast.zl_ref, bf16[4,512,128]{2,1,0:T(8,128)(2,1)S(1)} %pad_maximum_fusion.q_ref, bf16[2,2,256,128]{3,2,1,0:T(8,128)(2,1)S(1)} %collective-permute-done.14.refs_0_, bf16[2,2,256,128]{3,2,1,0:T(8,128)(2,1)S(1)} %collective-permute-done.16.refs_1_, ...), custom_call_target="tpu_custom_call" | custom-call | flops 4294967296 | bytes 1048576 | tf_op jit(solution)/shard_map/flash/pallas_call | solution.py:128
  77.0 4.3 %flash.11 = (f32[8,2048]{1,0:T(8,128)S(1)}, f32[144,2048]{1,0:T(8,128)S(1)}) custom-call(s32[1]{0:T(128)} %bitcast.zl_ref, bf16[4,512,128]{2,1,0:T(8,128)(2,1)S(1)} %pad_maximum_fusion.q_ref, bf16[4,2,256,128]{3,2,1,0:T(8,128)(2,1)S(1)} %pad_maximum_fusion.1.refs_0_, f32[8,2048]{1,0:T(8,128)S(1)} %get-tuple-element.47.refs_1_, ...), custom_call_target="tpu_custom_call" | custom-call | flops 4294967296 | bytes 1048576 | tf_op jit(solution)/shard_map/flash/pallas_call | solution.py:128
  81.3 7.4 %flash.12 = (f32[8,2048]{1,0:T(8,128)S(1)}, f32[144,2048]{1,0:T(8,128)S(1)}) custom-call(s32[1]{0:T(128)} %bitcast.zl_ref, bf16[4,512,128]{2,1,0:T(8,128)(2,1)S(1)} %pad_maximum_fusion.q_ref, bf16[4,2,256,128]{3,2,1,0:T(8,128)(2,1)S(1)} %collective-permute-done.6.refs_0_, bf16[4,2,256,128]{3,2,1,0:T(8,128)(2,1)S(1)} %collective-permute-done.8.refs_1_, ...), custom_call_target="tpu_custom_call" | custom-call | flops 8589934592 | bytes 1572864 | tf_op jit(solution)/shard_map/flash/pallas_call | solution.py:128
  88.7 4.6 %flash.13 = bf16[4,512,128]{2,1,0:T(8,128)(2,1)S(1)} custom-call(s32[1]{0:T(128)} %bitcast.zl_ref, bf16[4,512,128]{2,1,0:T(8,128)(2,1)S(1)} %pad_maximum_fusion.q_ref, bf16[2,2,256,128]{3,2,1,0:T(8,128)(2,1)S(1)} %collective-permute-done.7.refs_0_, bf16[2,2,256,128]{3,2,1,0:T(8,128)(2,1)S(1)} %collective-permute-done.9.refs_1_, ...), custom_call_target="tpu_custom_call" | custom-call | flops 4294967296 | bytes 1048576 | tf_op jit(solution)/shard_map/flash/pallas_call | solution.py:128
  93.4 29.6 %all_to_all.5 = bf16[64,32,128]{2,1,0:T(8,128)(2,1)S(1)} all-to-all(bf16[64,32,128]{2,1,0:T(8,128)(2,1)S(1)} %bitcast.27), channel_id=1, replica_groups=mesh['zl'=4,'x'=4,'y'=4,'zh'=2,'c'=2] {'zl','y','zh','c'}, dimensions={0} | all-to-all | bytes 1048576 | tf_op jit(solution)/shard_map/all_to_all | solution.py:187
  123.5 0.9 reshape.27
  (27 shorter events, 1.8 us)
Async XLA Ops:
  0.0 1.2 copy-start
  0.0 1.4 %copy-start.1 = (bf16[512,2,256]{2,1,0:T(2,128)(2,1)S(1)}, bf16[512,2,256]{2,1,0:T(2,128)(2,1)}, u32[]{:S(2)}) copy-start(bf16[512,2,256]{2,1,0:T(2,128)(2,1)} %param.5) | copy-start | bytes 1572868
  1.7 11.0 %collective-permute-start.10 = (bf16[2,256,128]{2,1,0:T(8,128)(2,1)S(1)}, bf16[2,256,128]{2,1,0:T(8,128)(2,1)S(1)}, u32[]{:S(2)}, u32[]{:S(2)}) collective-permute-start(bf16[2,256,128]{2,1,0:T(8,128)(2,1)S(1)} %get-tuple-element.38), channel_id=1, source_target_pairs={{0,64},{64,128},{128,192},{192,0},{1,65},{65,129},{129,193},{193,1... | collective-permute-start | bytes 393224 | tf_op jit(solution)/shard_map/ppermute | solution.py:151
  3.7 17.4 %collective-permute-start.11 = (bf16[2,256,128]{2,1,0:T(8,128)(2,1)S(1)}, bf16[2,256,128]{2,1,0:T(8,128)(2,1)S(1)}, u32[]{:S(2)}, u32[]{:S(2)}) collective-permute-start(bf16[2,256,128]{2,1,0:T(8,128)(2,1)S(1)} %get-tuple-element.39), channel_id=1, source_target_pairs={{0,128},{64,192},{128,0},{192,64},{1,129},{65,193},{129,1},{193,65... | collective-permute-start | bytes 393224 | tf_op jit(solution)/shard_map/ppermute | solution.py:151
  6.0 18.1 %collective-permute-start.12 = (bf16[2,256,128]{2,1,0:T(8,128)(2,1)S(1)}, bf16[2,256,128]{2,1,0:T(8,128)(2,1)S(1)}, u32[]{:S(2)}, u32[]{:S(2)}) collective-permute-start(bf16[2,256,128]{2,1,0:T(8,128)(2,1)S(1)} %get-tuple-element.40), channel_id=1, source_target_pairs={{0,192},{64,0},{128,64},{192,128},{1,193},{65,1},{129,65},{193,129... | collective-permute-start | bytes 393224 | tf_op jit(solution)/shard_map/ppermute | solution.py:151
  7.1 17.9 %collective-permute-start.3 = (bf16[2,256,128]{2,1,0:T(8,128)(2,1)S(1)}, bf16[2,256,128]{2,1,0:T(8,128)(2,1)S(1)}, u32[]{:S(2)}, u32[]{:S(2)}) collective-permute-start(bf16[2,256,128]{2,1,0:T(8,128)(2,1)S(1)} %get-tuple-element.34), channel_id=1, source_target_pairs={{0,64},{64,128},{128,192},{192,0},{1,65},{65,129},{129,193},{193,1... | collective-permute-start | bytes 393224 | tf_op jit(solution)/shard_map/ppermute | solution.py:151
  8.0 24.9 %collective-permute-start.4 = (bf16[2,256,128]{2,1,0:T(8,128)(2,1)S(1)}, bf16[2,256,128]{2,1,0:T(8,128)(2,1)S(1)}, u32[]{:S(2)}, u32[]{:S(2)}) collective-permute-start(bf16[2,256,128]{2,1,0:T(8,128)(2,1)S(1)} %get-tuple-element.35), channel_id=1, source_target_pairs={{0,128},{64,192},{128,0},{192,64},{1,129},{65,193},{129,1},{193,65... | collective-permute-start | bytes 393224 | tf_op jit(solution)/shard_map/ppermute | solution.py:151
  12.7 21.7 %collective-permute-start.5 = (bf16[2,256,128]{2,1,0:T(8,128)(2,1)S(1)}, bf16[2,256,128]{2,1,0:T(8,128)(2,1)S(1)}, u32[]{:S(2)}, u32[]{:S(2)}) collective-permute-start(bf16[2,256,128]{2,1,0:T(8,128)(2,1)S(1)} %get-tuple-element.36), channel_id=1, source_target_pairs={{0,192},{64,0},{128,64},{192,128},{1,193},{65,1},{129,65},{193,129... | collective-permute-start | bytes 393224 | tf_op jit(solution)/shard_map/ppermute | solution.py:151
  21.2 15.7 %collective-permute-start = (bf16[512,128]{1,0:T(8,128)(2,1)S(1)}, bf16[512,128]{1,0:T(8,128)(2,1)S(1)}, u32[]{:S(2)}, u32[]{:S(2)}) collective-permute-start(bf16[512,128]{1,0:T(8,128)(2,1)S(1)} %get-tuple-element.30), channel_id=1, source_target_pairs={{0,64},{64,128},{128,192},{192,0},{1,65},{65,129},{129,193},{193,1... | collective-permute-start | bytes 393224 | tf_op jit(solution)/shard_map/ppermute | solution.py:151
  24.1 13.3 %collective-permute-start.1 = (bf16[512,128]{1,0:T(8,128)(2,1)S(1)}, bf16[512,128]{1,0:T(8,128)(2,1)S(1)}, u32[]{:S(2)}, u32[]{:S(2)}) collective-permute-start(bf16[512,128]{1,0:T(8,128)(2,1)S(1)} %get-tuple-element.31), channel_id=1, source_target_pairs={{0,128},{64,192},{128,0},{192,64},{1,129},{65,193},{129,1},{193,65... | collective-permute-start | bytes 393224 | tf_op jit(solution)/shard_map/ppermute | solution.py:151
  25.0 15.2 %collective-permute-start.2 = (bf16[512,128]{1,0:T(8,128)(2,1)S(1)}, bf16[512,128]{1,0:T(8,128)(2,1)S(1)}, u32[]{:S(2)}, u32[]{:S(2)}) collective-permute-start(bf16[512,128]{1,0:T(8,128)(2,1)S(1)} %get-tuple-element.32), channel_id=1, source_target_pairs={{0,192},{64,0},{128,64},{192,128},{1,193},{65,1},{129,65},{193,129... | collective-permute-start | bytes 393224 | tf_op jit(solution)/shard_map/ppermute | solution.py:151
  32.9 13.3 %collective-permute-start.13 = (bf16[4,2,256,128]{3,2,1,0:T(8,128)(2,1)S(1)}, bf16[4,2,256,128]{3,2,1,0:T(8,128)(2,1)S(1)}, u32[]{:S(2)}, u32[]{:S(2)}) collective-permute-start(bf16[4,2,256,128]{3,2,1,0:T(8,128)(2,1)S(1)} %pad_maximum_fusion.2.refs_0_), channel_id=1, source_target_pairs={{0,16},{16,32},{32,48},{48,0},{1,17},{17,33},{33,49},{49,1},{2,18}... | collective-permute-start | bytes 1572872 | tf_op jit(solution)/shard_map/ppermute | solution.py:151
  34.4 14.8 %collective-permute-start.15 = (bf16[4,2,256,128]{3,2,1,0:T(8,128)(2,1)S(1)}, bf16[4,2,256,128]{3,2,1,0:T(8,128)(2,1)S(1)}, u32[]{:S(2)}, u32[]{:S(2)}) collective-permute-start(bf16[4,2,256,128]{3,2,1,0:T(8,128)(2,1)S(1)} %pad_maximum_fusion.2.refs_0_), channel_id=1, source_target_pairs={{0,48},{16,0},{32,16},{48,32},{1,49},{17,1},{33,17},{49,33},{2,50}... | collective-permute-start | bytes 1572872 | tf_op jit(solution)/shard_map/ppermute | solution.py:151
  36.9 20.5 %collective-permute-start.6 = (bf16[4,2,256,128]{3,2,1,0:T(8,128)(2,1)S(1)}, bf16[4,2,256,128]{3,2,1,0:T(8,128)(2,1)S(1)}, u32[]{:S(2)}, u32[]{:S(2)}) collective-permute-start(bf16[4,2,256,128]{3,2,1,0:T(8,128)(2,1)S(1)} %pad_maximum_fusion.1.refs_0_), channel_id=1, source_target_pairs={{0,16},{16,32},{32,48},{48,0},{1,17},{17,33},{33,49},{49,1},{2,18}... | collective-permute-start | bytes 1572872 | tf_op jit(solution)/shard_map/ppermute | solution.py:151
  37.4 23.0 %collective-permute-start.8 = (bf16[4,2,256,128]{3,2,1,0:T(8,128)(2,1)S(1)}, bf16[4,2,256,128]{3,2,1,0:T(8,128)(2,1)S(1)}, u32[]{:S(2)}, u32[]{:S(2)}) collective-permute-start(bf16[4,2,256,128]{3,2,1,0:T(8,128)(2,1)S(1)} %pad_maximum_fusion.1.refs_0_), channel_id=1, source_target_pairs={{0,48},{16,0},{32,16},{48,32},{1,49},{17,1},{33,17},{49,33},{2,50}... | collective-permute-start | bytes 1572872 | tf_op jit(solution)/shard_map/ppermute | solution.py:151
  46.2 26.5 %collective-permute-start.14 = (bf16[2,2,256,128]{3,2,1,0:T(8,128)(2,1)S(1)}, bf16[2,2,256,128]{3,2,1,0:T(8,128)(2,1)S(1)}, u32[]{:S(2)}, u32[]{:S(2)}) collective-permute-start(bf16[2,2,256,128]{3,2,1,0:T(8,128)(2,1)S(1)} %slice.18), channel_id=1, source_target_pairs={{0,16},{16,32},{32,48},{48,0},{1,17},{17,33},{33,49},{49,1},{2,18}... | collective-permute-start | bytes 786440 | tf_op jit(solution)/shard_map/ppermute | solution.py:151
  49.2 23.5 %collective-permute-start.16 = (bf16[2,2,256,128]{3,2,1,0:T(8,128)(2,1)S(1)}, bf16[2,2,256,128]{3,2,1,0:T(8,128)(2,1)S(1)}, u32[]{:S(2)}, u32[]{:S(2)}) collective-permute-start(bf16[2,2,256,128]{3,2,1,0:T(8,128)(2,1)S(1)} %slice.19), channel_id=1, source_target_pairs={{0,48},{16,0},{32,16},{48,32},{1,49},{17,1},{33,17},{49,33},{2,50}... | collective-permute-start | bytes 786440 | tf_op jit(solution)/shard_map/ppermute | solution.py:151
  57.4 31.3 %collective-permute-start.7 = (bf16[2,2,256,128]{3,2,1,0:T(8,128)(2,1)S(1)}, bf16[2,2,256,128]{3,2,1,0:T(8,128)(2,1)S(1)}, u32[]{:S(2)}, u32[]{:S(2)}) collective-permute-start(bf16[2,2,256,128]{3,2,1,0:T(8,128)(2,1)S(1)} %slice.16), channel_id=1, source_target_pairs={{0,16},{16,32},{32,48},{48,0},{1,17},{17,33},{33,49},{49,1},{2,18}... | collective-permute-start | bytes 786440 | tf_op jit(solution)/shard_map/ppermute | solution.py:151
  60.5 28.3 %collective-permute-start.9 = (bf16[2,2,256,128]{3,2,1,0:T(8,128)(2,1)S(1)}, bf16[2,2,256,128]{3,2,1,0:T(8,128)(2,1)S(1)}, u32[]{:S(2)}, u32[]{:S(2)}) collective-permute-start(bf16[2,2,256,128]{3,2,1,0:T(8,128)(2,1)S(1)} %slice.17), channel_id=1, source_target_pairs={{0,48},{16,0},{32,16},{48,32},{1,49},{17,1},{33,17},{49,33},{2,50}... | collective-permute-start | bytes 786440 | tf_op jit(solution)/shard_map/ppermute | solution.py:151

commit v2 on v1

--- a/solution.py
+++ b/solution.py
@@ -20,7 +20,7 @@
 def pack_kernel(zl_ref, q_ref, k_ref, v_ref, *out_refs):
     for s in range(4):
         q_out, c0_out, c1_out = out_refs[3 * s:3 * s + 3]
-        at = pl.multiple_of(lax.rem(zl_ref[0] + s, 4) * HEAD_DIM, HEAD_DIM)
+        at = pl.multiple_of((zl_ref[0] ^ s) * HEAD_DIM, HEAD_DIM)
         head = pl.ds(at, HEAD_DIM)
         q_out[...] = q_ref[:, head]
         c0_out[0] = k_ref[0:PIECE, head]
@@ -46,7 +46,7 @@
     return outs[0::3], outs[1::3], outs[2::3]
 
 
-def flash_kernel(first, last, counts, zl_ref, q_ref, *refs):
+def flash_kernel(first, last, counts, at_ref, q_ref, *refs):
     kv_refs, refs = refs[: len(counts)], refs[len(counts):]
     if not first:
         peak_in, acc_in, *refs = refs
@@ -90,46 +90,47 @@
         peak, scores = new_peak, following
     if last:
         attended = acc[0:HEAD_DIM, :] / acc[HEAD_DIM:HEAD_DIM + 1, :]
-        out_ref[0] = attended.T.astype(jnp.bfloat16)
+        rows = attended.T.astype(jnp.bfloat16).reshape(8, 2, tile // 16, HEAD_DIM)
+        for core in range(2):
+            out_ref[0, :, core ^ at_ref[1]] = rows[:, core]
     else:
         peak_out[...] = jnp.broadcast_to(peak, peak_out.shape)
         acc_out[...] = acc
 
 
-def flash(zl, queries, blocks, state, last):
-    sources, rows, _ = queries.shape
-    per_source = rows // Q_TILE
-    total = sources * rows
+def flash(at, queries, blocks, state, last):
+    tiles = queries.shape[0]
     counts = tuple(b.shape[0] for b in blocks)
     first = state is None
-    q_spec = pl.BlockSpec((1, Q_TILE, HEAD_DIM), lambda i, z: (i // per_source, i % per_source, 0))
+    q_spec = pl.BlockSpec((1, Q_TILE, HEAD_DIM), lambda i, at: (i, 0, 0))
     in_specs = [q_spec] + [
-        pl.BlockSpec((c, 2, PIECE, HEAD_DIM), lambda i, z: (0, 0, 0, 0)) for c in counts
+        pl.BlockSpec((c, 2, PIECE, HEAD_DIM), lambda i, at: (0, 0, 0, 0)) for c in counts
     ]
-    peak_spec = pl.BlockSpec((8, Q_TILE), lambda i, z: (0, i))
-    acc_spec = pl.BlockSpec((HEAD_DIM + SUM_ROWS, Q_TILE), lambda i, z: (0, i))
+    peak_spec = pl.BlockSpec((8, Q_TILE), lambda i, at: (0, i))
+    acc_spec = pl.BlockSpec((HEAD_DIM + SUM_ROWS, Q_TILE), lambda i, at: (0, i))
     args = [queries, *blocks]
     if not first:
         in_specs += [peak_spec, acc_spec]
         args += list(state)
     if last:
+        strip = Q_TILE // 16
         out_specs = pl.BlockSpec(
-            (1, Q_TILE, HEAD_DIM),
-            lambda i, z: (lax.rem(z[0] + 4 - i // per_source, 4), i % per_source, 0),
+            (1, 8, 2, strip, HEAD_DIM), lambda i, at: (at[0] ^ i, 0, 0, 0, 0)
         )
-        out_shape = jax.ShapeDtypeStruct(queries.shape, jnp.bfloat16)
+        out_shape = jax.ShapeDtypeStruct((tiles, 8, 2, strip, HEAD_DIM), jnp.bfloat16)
     else:
         out_specs = [peak_spec, acc_spec]
         out_shape = [
-            jax.ShapeDtypeStruct((8, total), jnp.float32),
-            jax.ShapeDtypeStruct((HEAD_DIM + SUM_ROWS, total), jnp.float32),
+            jax.ShapeDtypeStruct((8, tiles * Q_TILE), jnp.float32),
+            jax.ShapeDtypeStruct((HEAD_DIM + SUM_ROWS, tiles * Q_TILE), jnp.float32),
         ]
     key_count = sum(counts) * PIECE
+    total = tiles * Q_TILE
     return pl.pallas_call(
         partial(flash_kernel, first, last, counts),
         grid_spec=pltpu.PrefetchScalarGridSpec(
             num_scalar_prefetch=1,
-            grid=(total // Q_TILE,),
+            grid=(tiles,),
             in_specs=in_specs,
             out_specs=out_specs,
             scratch_shapes=[pltpu.VMEM((HEAD_DIM + SUM_ROWS, key_count), jnp.bfloat16)],
@@ -144,49 +145,76 @@
             transcendentals=total * key_count,
         ),
         name="flash",
-    )(zl, *args)
-
-
-def shift(array, axis, by):
-    return lax.ppermute(array, axis, [(i, (i + by) % 4) for i in range(4)])
+    )(at, *args)
+
+
+def gate_kernel(in_ref, out_ref):
+    out_ref[0] = in_ref[0]
+    out_ref[1] = in_ref[1]
+
+
+def gate(position):
+    return pl.pallas_call(
+        gate_kernel,
+        in_specs=[pl.BlockSpec(memory_space=pltpu.SMEM)],
+        out_specs=pl.BlockSpec(memory_space=pltpu.SMEM),
+        out_shape=jax.ShapeDtypeStruct((2,), jnp.int32),
+        compiler_params=pltpu.CompilerParams(vmem_limit_bytes=VMEM_BYTES),
+        name="gate",
+    )(position)
+
+
+def shift(array, by):
+    return lax.ppermute(array, "x", [(i, (i + by) % 4) for i in range(4)])
 
 
 def to_heads(packed):
     parts = [packed[0]]
     for s in (1, 2, 3):
-        parts.append(shift(packed[s], "zl", s))
+        parts.append(lax.ppermute(packed[s], "zl", [(i, i ^ s) for i in range(4)]))
     return jnp.stack(parts)
 
 
-def around_ring(block):
-    left = shift(block, "x", 1)
-    right = shift(block, "x", -1)
-    half = block.shape[0] // 2
-    far_a = shift(left[:half], "x", 1)
-    far_b = shift(right[half:], "x", -1)
-    return left, right, [far_a, far_b]
+def neighbours(block):
+    left = shift(block, 1)
+    right = shift(block, -1)
+    return [left, right]
+
+
+def forwarded(near0, near1):
+    half = near0[0].shape[0] // 2
+    far_a = shift(jnp.concatenate([near0[0][:half], near1[0][:half]]), 1)
+    far_b = shift(jnp.concatenate([near0[1][half:], near1[1][half:]]), -1)
+    return [far_a, far_b]
 
 
 def attention(queries, keys, values):
     rows = queries.shape[0]
-    zl = lax.axis_index("zl").astype(jnp.int32).reshape(1)
-    q_packed, c0, c1 = pack_heads(zl, queries, keys, values)
+    position = jnp.stack([lax.axis_index("zl"), lax.axis_index("c")]).astype(jnp.int32)
+    q_packed, c0, c1 = pack_heads(position, queries, keys, values)
     own0 = to_heads(c0)
+    own1 = to_heads(c1)
     q_all = to_heads(q_packed)
-    own1 = to_heads(c1)
-    left0, right0, far0 = around_ring(own0)
-    left1, right1, far1 = around_ring(own1)
-    steps = [
-        ("own0", [own0]), ("left0", [left0]), ("right0", [right0]), ("far0", far0),
-        ("own1", [own1]), ("near1", [left1, right1]), ("far1", far1),
-    ]
+    near0 = neighbours(own0)
+    near1 = neighbours(own1)
+    far = forwarded(near0, near1)
     state = None
-    for name, blocks in steps:
-        state = flash(zl, q_all, blocks, state, name == "far1")
-    blocks = state.reshape(64, rows // 16, HEAD_DIM)
-    blocks = lax.all_to_all(blocks, ("zl", "y", "zh", "c"), 0, 0, tiled=True)
-    out = blocks.reshape(2, 2, 16, rows // 16, HEAD_DIM).transpose(3, 0, 2, 1, 4)
-    return out.reshape(rows // 16, 2, 32 * HEAD_DIM)
+    at = gate(position)
+    for name, blocks in (("1", [own0, *near0]), ("2", [own1, *near1]), ("3", far)):
+        state = flash(at, q_all, blocks, state, name == "3")
+    return to_tokens(state, rows // 16)
+
+
+def to_tokens(attended, strip):
+    blocks = attended.reshape(32, 2 * strip, HEAD_DIM)
+    blocks = lax.all_to_all(blocks, ("zl", "y", "zh"), 0, 0, tiled=True)
+    blocks = blocks.reshape(32, 2, strip, HEAD_DIM)
+    own = blocks[:, 0]
+    other = lax.ppermute(blocks[:, 1], "c", [(0, 1), (1, 0)])
+    first = lax.axis_index("c") == 0
+    both = jnp.stack([jnp.where(first, own, other), jnp.where(first, other, own)], axis=1)
+    out = both.reshape(2, 2, 16, strip, HEAD_DIM).transpose(3, 0, 2, 1, 4)
+    return out.reshape(strip, 2, 32 * HEAD_DIM)
 
 
 def solution(mesh):

time: 126 us -> 118 us (0.937)
  starting transfers between devices: 29.5 us -> 20 us
  waiting for transfers between devices: 28.6 us -> 35 us
  blocking collectives: 29.6 us -> 27.1 us
  Pallas kernels: 33.5 us -> 31.6 us
    ppermute x17 -> x16, starting transfers between devices: 29.5 us -> 20 us  [the longest x9 11.1 us: to_heads(): parts.append(lax.ppermute(packed[s], 'zl', [(i, i ^ s) for i in range(4)]))]
    ppermute x17 -> x16, waiting for transfers between devices: 28.6 us -> 35 us  [the longest x9 27.4 us: to_heads(): parts.append(lax.ppermute(packed[s], 'zl', [(i, i ^ s) for i in range(4)]))]
    pallas_call x7 -> x3, Pallas kernels: 33.2 us -> 29.7 us  [flash(): pl.pallas_call(partial(flash_kernel, first, last, counts), grid_spec=pltp...]
    all_to_all x1, blocking collectives: 29.6 us -> 27.1 us  [to_tokens(): blocks = lax.all_to_all(blocks, ('zl', 'y', 'zh'), 0, 0, tiled=True)]
  transfers between devices with their start and end apart: 17 -> 16, of which waited for: 9 -> 8; matrix products, arithmetic and copies ran while one was open for 0% -> 0% of each run, Pallas kernels for 23% -> 19%
where the time goes in v2:
time: 118 us; the launch traced here: 117 us
  waiting for transfers between devices  35 us (30%)
  Pallas kernels  31.6 us (27%)
  blocking collectives  27.1 us (23%)
  starting transfers between devices  20 us (17%)
  local copies, waits for them, and re-layouts  3.02 us (3%)
    pallas_call x3, Pallas kernels, flash(): pl.pallas_call(partial(flash_kernel, first, last, counts), grid_spec=pltp...  29.7 us
    ppermute x9, waiting for transfers between devices, to_heads(): parts.append(lax.ppermute(packed[s], 'zl', [(i, i ^ s) for i in range(4)]))  27.4 us
    all_to_all x1, blocking collectives, to_tokens(): blocks = lax.all_to_all(blocks, ('zl', 'y', 'zh'), 0, 0, tiled=True)  27.1 us
    ppermute x9, starting transfers between devices, to_heads(): parts.append(lax.ppermute(packed[s], 'zl', [(i, i ^ s) for i in range(4)]))  11.1 us
    ppermute x6, starting transfers between devices, shift(): return lax.ppermute(array, 'x', [(i, (i + by) % 4) for i in range(4)])  8.83 us
    ppermute x6, waiting for transfers between devices, shift(): return lax.ppermute(array, 'x', [(i, (i + by) % 4) for i in range(4)])  6.1 us
  transfers between devices with their start and end apart: 16, of which 8 were waited for; matrix products, arithmetic and copies ran while one was open for 0% of the time, Pallas kernels for 19%

profile of v2, /device:TPU:32, one launch (start us, length us, event | category | flops | bytes accessed | tf_op | source)
XLA Modules:
  0.0 117.5 jit_solution(16654515692606257177)
XLA Ops:
  0.0 1.2 %copy.13 = bf16[64,8,2,256]{3,1,2,0:T(8,128)(2,1)S(1)} copy(bf16[64,8,2,256]{3,2,1,0:T(2,128)(2,1)} %bitcast.49) | data formatting | bytes 1048576
  1.2 0.1 copy.14
  1.5 0.8 pack.1
  2.4 1.9 %collective-permute-start.3 = (bf16[2,256,128]{2,1,0:T(8,128)(2,1)S(1)}, bf16[2,256,128]{2,1,0:T(8,128)(2,1)S(1)}, u32[]{:S(2)}, u32[]{:S(2)}) collective-permute-start(bf16[2,256,128]{2,1,0:T(8,128)(2,1)S(1)} %get-tuple-element.26), channel_id=1, source_target_pairs={{0,64},{64,0},{128,192},{192,128},{1,65},{65,1},{129,193},{193,129... | collective-permute-start | bytes 393224 | tf_op jit(solution)/shard_map/ppermute | solution.py:174
  4.3 1.6 %collective-permute-start.4 = (bf16[2,256,128]{2,1,0:T(8,128)(2,1)S(1)}, bf16[2,256,128]{2,1,0:T(8,128)(2,1)S(1)}, u32[]{:S(2)}, u32[]{:S(2)}) collective-permute-start(bf16[2,256,128]{2,1,0:T(8,128)(2,1)S(1)} %get-tuple-element.27), channel_id=1, source_target_pairs={{0,128},{64,192},{128,0},{192,64},{1,129},{65,193},{129,1},{193,65... | collective-permute-start | bytes 393224 | tf_op jit(solution)/shard_map/ppermute | solution.py:174
  5.8 0.5 collective-permute-start.5
  6.3 2.4 %collective-permute-start.7 = (bf16[2,256,128]{2,1,0:T(8,128)(2,1)S(1)}, bf16[2,256,128]{2,1,0:T(8,128)(2,1)S(1)}, u32[]{:S(2)}, u32[]{:S(2)}) collective-permute-start(bf16[2,256,128]{2,1,0:T(8,128)(2,1)S(1)} %get-tuple-element.30), channel_id=1, source_target_pairs={{0,64},{64,0},{128,192},{192,128},{1,65},{65,1},{129,193},{193,129... | collective-permute-start | bytes 393224 | tf_op jit(solution)/shard_map/ppermute | solution.py:174
  8.6 1.5 %collective-permute-start.8 = (bf16[2,256,128]{2,1,0:T(8,128)(2,1)S(1)}, bf16[2,256,128]{2,1,0:T(8,128)(2,1)S(1)}, u32[]{:S(2)}, u32[]{:S(2)}) collective-permute-start(bf16[2,256,128]{2,1,0:T(8,128)(2,1)S(1)} %get-tuple-element.31), channel_id=1, source_target_pairs={{0,128},{64,192},{128,0},{192,64},{1,129},{65,193},{129,1},{193,65... | collective-permute-start | bytes 393224 | tf_op jit(solution)/shard_map/ppermute | solution.py:174
  10.1 0.7 collective-permute-start.9
  10.8 5.5 %collective-permute-done.4 = bf16[2,256,128]{2,1,0:T(8,128)(2,1)S(1)} collective-permute-done((bf16[2,256,128]{2,1,0:T(8,128)(2,1)S(1)}, bf16[2,256,128]{2,1,0:T(8,128)(2,1)S(1)}, u32[]{:S(2)}, u32[]{:S(2)}) %collective-permute-start.4) | collective-permute-done | bytes 131104 | tf_op jit(solution)/shard_map/ppermute | solution.py:174
  16.3 8.4 %collective-permute-done.5 = bf16[2,256,128]{2,1,0:T(8,128)(2,1)S(1)} collective-permute-done((bf16[2,256,128]{2,1,0:T(8,128)(2,1)S(1)}, bf16[2,256,128]{2,1,0:T(8,128)(2,1)S(1)}, u32[]{:S(2)}, u32[]{:S(2)}) %collective-permute-start.5) | collective-permute-done | bytes 131104 | tf_op jit(solution)/shard_map/ppermute | solution.py:174
  24.8 2.8 %collective-permute-start.12 = (bf16[4,2,256,128]{3,2,1,0:T(8,128)(2,1)S(1)}, bf16[4,2,256,128]{3,2,1,0:T(8,128)(2,1)S(1)}, u32[]{:S(2)}, u32[]{:S(2)}) collective-permute-start(bf16[4,2,256,128]{3,2,1,0:T(8,128)(2,1)S(1)} %pad_maximum_fusion.1.refs_0_), channel_id=1, source_target_pairs={{0,48},{16,0},{32,16},{48,32},{1,49},{17,1},{33,17},{49,33},{2,50}... | collective-permute-start | bytes 1572872 | tf_op jit(solution)/shard_map/ppermute | solution.py:168
  27.6 1.7 %collective-permute-done.9 = bf16[2,256,128]{2,1,0:T(8,128)(2,1)S(1)} collective-permute-done((bf16[2,256,128]{2,1,0:T(8,128)(2,1)S(1)}, bf16[2,256,128]{2,1,0:T(8,128)(2,1)S(1)}, u32[]{:S(2)}, u32[]{:S(2)}) %collective-permute-start.9) | collective-permute-done | bytes 131104 | tf_op jit(solution)/shard_map/ppermute | solution.py:174
  29.3 2.8 %collective-permute-start.13 = (bf16[4,2,256,128]{3,2,1,0:T(8,128)(2,1)S(1)}, bf16[4,2,256,128]{3,2,1,0:T(8,128)(2,1)S(1)}, u32[]{:S(2)}, u32[]{:S(2)}) collective-permute-start(bf16[4,2,256,128]{3,2,1,0:T(8,128)(2,1)S(1)} %pad_maximum_fusion.2.refs_0_), channel_id=1, source_target_pairs={{0,48},{16,0},{32,16},{48,32},{1,49},{17,1},{33,17},{49,33},{2,50}... | collective-permute-start | bytes 1572872 | tf_op jit(solution)/shard_map/ppermute | solution.py:168
  32.1 0.8 collective-permute-start.10
  32.8 4.2 %collective-permute-done = bf16[512,128]{1,0:T(8,128)(2,1)S(1)} collective-permute-done((bf16[512,128]{1,0:T(8,128)(2,1)S(1)}, bf16[512,128]{1,0:T(8,128)(2,1)S(1)}, u32[]{:S(2)}, u32[]{:S(2)}) %collective-permute-start) | collective-permute-done | bytes 131104 | tf_op jit(solution)/shard_map/ppermute | solution.py:174
  37.0 1.1 collective-permute-start.1
  38.1 4.9 %collective-permute-done.1 = bf16[512,128]{1,0:T(8,128)(2,1)S(1)} collective-permute-done((bf16[512,128]{1,0:T(8,128)(2,1)S(1)}, bf16[512,128]{1,0:T(8,128)(2,1)S(1)}, u32[]{:S(2)}, u32[]{:S(2)}) %collective-permute-start.1) | collective-permute-done | bytes 131104 | tf_op jit(solution)/shard_map/ppermute | solution.py:174
  43.0 1.6 %collective-permute-start.2 = (bf16[512,128]{1,0:T(8,128)(2,1)S(1)}, bf16[512,128]{1,0:T(8,128)(2,1)S(1)}, u32[]{:S(2)}, u32[]{:S(2)}) collective-permute-start(bf16[512,128]{1,0:T(8,128)(2,1)S(1)} %get-tuple-element.24), channel_id=1, source_target_pairs={{0,192},{64,128},{128,64},{192,0},{1,193},{65,129},{129,65},{193,1... | collective-permute-start | bytes 393224 | tf_op jit(solution)/shard_map/ppermute | solution.py:174
  44.6 1.1 gate.1.at_ref
  45.7 2.7 %collective-permute-done.2 = bf16[512,128]{1,0:T(8,128)(2,1)S(1)} collective-permute-done((bf16[512,128]{1,0:T(8,128)(2,1)S(1)}, bf16[512,128]{1,0:T(8,128)(2,1)S(1)}, u32[]{:S(2)}, u32[]{:S(2)}) %collective-permute-start.2) | collective-permute-done | bytes 131104 | tf_op jit(solution)/shard_map/ppermute | solution.py:174
  48.7 2.3 %collective-permute-start.14 = (bf16[4,2,256,128]{3,2,1,0:T(8,128)(2,1)S(1)}, bf16[4,2,256,128]{3,2,1,0:T(8,128)(2,1)S(1)}, u32[]{:S(2)}, u32[]{:S(2)}) collective-permute-start(bf16[4,2,256,128]{3,2,1,0:T(8,128)(2,1)S(1)} %pad_maximum_fusion.4), channel_id=1, source_target_pairs={{0,48},{16,0},{32,16},{48,32},{1,49},{17,1},{33,17},{49,33},{2,50}... | collective-permute-start | bytes 1572872 | tf_op jit(solution)/shard_map/ppermute | solution.py:168
  51.0 6.1 %collective-permute-done.10.refs_1_ = bf16[4,2,256,128]{3,2,1,0:T(8,128)(2,1)S(1)} collective-permute-done((bf16[4,2,256,128]{3,2,1,0:T(8,128)(2,1)S(1)}, bf16[4,2,256,128]{3,2,1,0:T(8,128)(2,1)S(1)}, u32[]{:S(2)}, u32[]{:S(2)}) %collective-permute-start.10) | collective-permute-done | bytes 524320 | tf_op jit(solution)/shard_map/ppermute | solution.py:168
  57.1 0.3 collective-permute-start.11
  57.4 10.4 %flash.3 = (f32[8,2048]{1,0:T(8,128)S(1)}, f32[144,2048]{1,0:T(8,128)S(1)}) custom-call(s32[2]{0:T(128)S(1)} %gate.1.at_ref, bf16[4,512,128]{2,1,0:T(8,128)(2,1)S(1)} %pad_maximum_fusion.q_ref, bf16[4,2,256,128]{3,2,1,0:T(8,128)(2,1)S(1)} %pad_maximum_fusion.1.refs_0_, bf16[4,2,256,128]{3,2,1,0:T(8,128)(2,1)S(1)} %collective-permute-done.6.refs_1_, ...), custom_call_target="tpu_custom_call" | custom-call | flops 12884901888 | bytes 2097152 | tf_op jit(solution)/shard_map/flash/pallas_call | solution.py:129
  67.8 10.9 %flash.4 = (f32[8,2048]{1,0:T(8,128)S(1)}, f32[144,2048]{1,0:T(8,128)S(1)}) custom-call(s32[2]{0:T(128)S(1)} %gate.1.at_ref, bf16[4,512,128]{2,1,0:T(8,128)(2,1)S(1)} %pad_maximum_fusion.q_ref, bf16[4,2,256,128]{3,2,1,0:T(8,128)(2,1)S(1)} %pad_maximum_fusion.2.refs_0_, bf16[4,2,256,128]{3,2,1,0:T(8,128)(2,1)S(1)} %collective-permute-done.10.refs_1_, ...), custom_call_target="tpu_custom_call" | custom-call | flops 12884901888 | bytes 2097152 | tf_op jit(solution)/shard_map/flash/pallas_call | solution.py:129
  78.7 8.3 %flash.5 = bf16[4,8,2,32,128]{4,3,2,1,0:T(8,128)(2,1)S(1)} custom-call(s32[2]{0:T(128)S(1)} %gate.1.at_ref, bf16[4,512,128]{2,1,0:T(8,128)(2,1)S(1)} %pad_maximum_fusion.q_ref, bf16[4,2,256,128]{3,2,1,0:T(8,128)(2,1)S(1)} %collective-permute-done.11.refs_0_, bf16[4,2,256,128]{3,2,1,0:T(8,128)(2,1)S(1)} %collective-permute-done.14.refs_1_, ...), custom_call_target="tpu_custom_call" | custom-call | flops 8589934592 | bytes 1572864 | tf_op jit(solution)/shard_map/flash/pallas_call | solution.py:129
  87.1 27.1 %all_to_all.5 = bf16[32,64,128]{2,1,0:T(8,128)(2,1)S(1)} all-to-all(bf16[32,64,128]{2,1,0:T(8,128)(2,1)S(1)} %bitcast.42), channel_id=1, replica_groups=mesh['zl'=4,'x'=4,'y'=4,'zh'=2,'c'=2] {'zl','y','zh'}, dimensions={0} | all-to-all | bytes 1048576 | tf_op jit(solution)/shard_map/all_to_all | solution.py:210
  114.2 0.1 collective-permute-start.15
  114.3 1.5 %collective-permute-done.15 = bf16[32,32,128]{2,1,0:T(8,128)(2,1)S(1)} collective-permute-done((bf16[32,32,128]{2,1,0:T(8,128)(2,1)S(1)}, bf16[32,32,128]{2,1,0:T(8,128)(2,1)S(1)}, u32[]{:S(2)}, u32[]{:S(2)}) %collective-permute-start.15) | collective-permute-done | bytes 262176 | tf_op jit(solution)/shard_map/ppermute | solution.py:213
  116.0 0.5 copy.10
  116.5 0.9 reshape.28
  (29 shorter events, 0.8 us)
Async XLA Ops:
  0.0 1.2 %copy-start = (bf16[512,2,256]{2,1,0:T(2,128)(2,1)S(1)}, bf16[512,2,256]{2,1,0:T(2,128)(2,1)}, u32[]{:S(2)}) copy-start(bf16[512,2,256]{2,1,0:T(2,128)(2,1)} %param.4) | copy-start | bytes 1572868
  0.0 1.4 %copy-start.1 = (bf16[512,2,256]{2,1,0:T(2,128)(2,1)S(1)}, bf16[512,2,256]{2,1,0:T(2,128)(2,1)}, u32[]{:S(2)}) copy-start(bf16[512,2,256]{2,1,0:T(2,128)(2,1)} %param.5) | copy-start | bytes 1572868
  2.4 7.8 %collective-permute-start.3 = (bf16[2,256,128]{2,1,0:T(8,128)(2,1)S(1)}, bf16[2,256,128]{2,1,0:T(8,128)(2,1)S(1)}, u32[]{:S(2)}, u32[]{:S(2)}) collective-permute-start(bf16[2,256,128]{2,1,0:T(8,128)(2,1)S(1)} %get-tuple-element.26), channel_id=1, source_target_pairs={{0,64},{64,0},{128,192},{192,128},{1,65},{65,1},{129,193},{193,129... | collective-permute-start | bytes 393224 | tf_op jit(solution)/shard_map/ppermute | solution.py:174
  4.3 12.0 %collective-permute-start.4 = (bf16[2,256,128]{2,1,0:T(8,128)(2,1)S(1)}, bf16[2,256,128]{2,1,0:T(8,128)(2,1)S(1)}, u32[]{:S(2)}, u32[]{:S(2)}) collective-permute-start(bf16[2,256,128]{2,1,0:T(8,128)(2,1)S(1)} %get-tuple-element.27), channel_id=1, source_target_pairs={{0,128},{64,192},{128,0},{192,64},{1,129},{65,193},{129,1},{193,65... | collective-permute-start | bytes 393224 | tf_op jit(solution)/shard_map/ppermute | solution.py:174
  5.8 18.9 %collective-permute-start.5 = (bf16[2,256,128]{2,1,0:T(8,128)(2,1)S(1)}, bf16[2,256,128]{2,1,0:T(8,128)(2,1)S(1)}, u32[]{:S(2)}, u32[]{:S(2)}) collective-permute-start(bf16[2,256,128]{2,1,0:T(8,128)(2,1)S(1)} %get-tuple-element.28), channel_id=1, source_target_pairs={{0,192},{64,128},{128,64},{192,0},{1,193},{65,129},{129,65},{193,1... | collective-permute-start | bytes 393224 | tf_op jit(solution)/shard_map/ppermute | solution.py:174
  6.3 21.3 %collective-permute-start.7 = (bf16[2,256,128]{2,1,0:T(8,128)(2,1)S(1)}, bf16[2,256,128]{2,1,0:T(8,128)(2,1)S(1)}, u32[]{:S(2)}, u32[]{:S(2)}) collective-permute-start(bf16[2,256,128]{2,1,0:T(8,128)(2,1)S(1)} %get-tuple-element.30), channel_id=1, source_target_pairs={{0,64},{64,0},{128,192},{192,128},{1,65},{65,1},{129,193},{193,129... | collective-permute-start | bytes 393224 | tf_op jit(solution)/shard_map/ppermute | solution.py:174
  8.6 18.9 %collective-permute-start.8 = (bf16[2,256,128]{2,1,0:T(8,128)(2,1)S(1)}, bf16[2,256,128]{2,1,0:T(8,128)(2,1)S(1)}, u32[]{:S(2)}, u32[]{:S(2)}) collective-permute-start(bf16[2,256,128]{2,1,0:T(8,128)(2,1)S(1)} %get-tuple-element.31), channel_id=1, source_target_pairs={{0,128},{64,192},{128,0},{192,64},{1,129},{65,193},{129,1},{193,65... | collective-permute-start | bytes 393224 | tf_op jit(solution)/shard_map/ppermute | solution.py:174
  10.1 19.1 %collective-permute-start.9 = (bf16[2,256,128]{2,1,0:T(8,128)(2,1)S(1)}, bf16[2,256,128]{2,1,0:T(8,128)(2,1)S(1)}, u32[]{:S(2)}, u32[]{:S(2)}) collective-permute-start(bf16[2,256,128]{2,1,0:T(8,128)(2,1)S(1)} %get-tuple-element.32), channel_id=1, source_target_pairs={{0,192},{64,128},{128,64},{192,0},{1,193},{65,129},{129,65},{193,1... | collective-permute-start | bytes 393224 | tf_op jit(solution)/shard_map/ppermute | solution.py:174
  24.8 23.8 %collective-permute-start.12 = (bf16[4,2,256,128]{3,2,1,0:T(8,128)(2,1)S(1)}, bf16[4,2,256,128]{3,2,1,0:T(8,128)(2,1)S(1)}, u32[]{:S(2)}, u32[]{:S(2)}) collective-permute-start(bf16[4,2,256,128]{3,2,1,0:T(8,128)(2,1)S(1)} %pad_maximum_fusion.1.refs_0_), channel_id=1, source_target_pairs={{0,48},{16,0},{32,16},{48,32},{1,49},{17,1},{33,17},{49,33},{2,50}... | collective-permute-start | bytes 1572872 | tf_op jit(solution)/shard_map/ppermute | solution.py:168
  29.3 19.3 %collective-permute-start.13 = (bf16[4,2,256,128]{3,2,1,0:T(8,128)(2,1)S(1)}, bf16[4,2,256,128]{3,2,1,0:T(8,128)(2,1)S(1)}, u32[]{:S(2)}, u32[]{:S(2)}) collective-permute-start(bf16[4,2,256,128]{3,2,1,0:T(8,128)(2,1)S(1)} %pad_maximum_fusion.2.refs_0_), channel_id=1, source_target_pairs={{0,48},{16,0},{32,16},{48,32},{1,49},{17,1},{33,17},{49,33},{2,50}... | collective-permute-start | bytes 1572872 | tf_op jit(solution)/shard_map/ppermute | solution.py:168
  32.1 5.0 %collective-permute-start = (bf16[512,128]{1,0:T(8,128)(2,1)S(1)}, bf16[512,128]{1,0:T(8,128)(2,1)S(1)}, u32[]{:S(2)}, u32[]{:S(2)}) collective-permute-start(bf16[512,128]{1,0:T(8,128)(2,1)S(1)} %get-tuple-element.22), channel_id=1, source_target_pairs={{0,64},{64,0},{128,192},{192,128},{1,65},{65,1},{129,193},{193,129... | collective-permute-start | bytes 393224 | tf_op jit(solution)/shard_map/ppermute | solution.py:174
  32.1 18.9 %collective-permute-start.6 = (bf16[4,2,256,128]{3,2,1,0:T(8,128)(2,1)S(1)}, bf16[4,2,256,128]{3,2,1,0:T(8,128)(2,1)S(1)}, u32[]{:S(2)}, u32[]{:S(2)}) collective-permute-start(bf16[4,2,256,128]{3,2,1,0:T(8,128)(2,1)S(1)} %pad_maximum_fusion.1.refs_0_), channel_id=1, source_target_pairs={{0,16},{16,32},{32,48},{48,0},{1,17},{17,33},{33,49},{49,1},{2,18}... | collective-permute-start | bytes 1572872 | tf_op jit(solution)/shard_map/ppermute | solution.py:168
  32.1 25.0 %collective-permute-start.10 = (bf16[4,2,256,128]{3,2,1,0:T(8,128)(2,1)S(1)}, bf16[4,2,256,128]{3,2,1,0:T(8,128)(2,1)S(1)}, u32[]{:S(2)}, u32[]{:S(2)}) collective-permute-start(bf16[4,2,256,128]{3,2,1,0:T(8,128)(2,1)S(1)} %pad_maximum_fusion.2.refs_0_), channel_id=1, source_target_pairs={{0,16},{16,32},{32,48},{48,0},{1,17},{17,33},{33,49},{49,1},{2,18}... | collective-permute-start | bytes 1572872 | tf_op jit(solution)/shard_map/ppermute | solution.py:168
  37.0 6.0 %collective-permute-start.1 = (bf16[512,128]{1,0:T(8,128)(2,1)S(1)}, bf16[512,128]{1,0:T(8,128)(2,1)S(1)}, u32[]{:S(2)}, u32[]{:S(2)}) collective-permute-start(bf16[512,128]{1,0:T(8,128)(2,1)S(1)} %get-tuple-element.23), channel_id=1, source_target_pairs={{0,128},{64,192},{128,0},{192,64},{1,129},{65,193},{129,1},{193,65... | collective-permute-start | bytes 393224 | tf_op jit(solution)/shard_map/ppermute | solution.py:174
  43.0 5.5 %collective-permute-start.2 = (bf16[512,128]{1,0:T(8,128)(2,1)S(1)}, bf16[512,128]{1,0:T(8,128)(2,1)S(1)}, u32[]{:S(2)}, u32[]{:S(2)}) collective-permute-start(bf16[512,128]{1,0:T(8,128)(2,1)S(1)} %get-tuple-element.24), channel_id=1, source_target_pairs={{0,192},{64,128},{128,64},{192,0},{1,193},{65,129},{129,65},{193,1... | collective-permute-start | bytes 393224 | tf_op jit(solution)/shard_map/ppermute | solution.py:174
  48.7 30.0 %collective-permute-start.14 = (bf16[4,2,256,128]{3,2,1,0:T(8,128)(2,1)S(1)}, bf16[4,2,256,128]{3,2,1,0:T(8,128)(2,1)S(1)}, u32[]{:S(2)}, u32[]{:S(2)}) collective-permute-start(bf16[4,2,256,128]{3,2,1,0:T(8,128)(2,1)S(1)} %pad_maximum_fusion.4), channel_id=1, source_target_pairs={{0,48},{16,0},{32,16},{48,32},{1,49},{17,1},{33,17},{49,33},{2,50}... | collective-permute-start | bytes 1572872 | tf_op jit(solution)/shard_map/ppermute | solution.py:168
  57.1 21.6 %collective-permute-start.11 = (bf16[4,2,256,128]{3,2,1,0:T(8,128)(2,1)S(1)}, bf16[4,2,256,128]{3,2,1,0:T(8,128)(2,1)S(1)}, u32[]{:S(2)}, u32[]{:S(2)}) collective-permute-start(bf16[4,2,256,128]{3,2,1,0:T(8,128)(2,1)S(1)} %pad_maximum_fusion.3), channel_id=1, source_target_pairs={{0,16},{16,32},{32,48},{48,0},{1,17},{17,33},{33,49},{49,1},{2,18}... | collective-permute-start | bytes 1572872 | tf_op jit(solution)/shard_map/ppermute | solution.py:168
  114.2 1.6 %collective-permute-start.15 = (bf16[32,32,128]{2,1,0:T(8,128)(2,1)S(1)}, bf16[32,32,128]{2,1,0:T(8,128)(2,1)S(1)}, u32[]{:S(2)}, u32[]{:S(2)}) collective-permute-start(bf16[32,32,128]{2,1,0:T(8,128)(2,1)S(1)} %slice_bitcast_fusion), channel_id=1, source_target_pairs={{0,1},{1,0},{2,3},{3,2},{4,5},{5,4},{6,7},{7,6},{8,9},{9,8},{10,11... | collective-permute-start | bytes 786440 | tf_op jit(solution)/shard_map/ppermute | solution.py:213
